TPU v7x, 32 devices: a whole 2x2x4 slice. The times are simulated.
32 devices in a mesh: wide: 8 (over z, core), narrow: 4 (over y, x).
Axes of the slice: x: 2, y: 2, z: 4, core: 2. Of those that a mesh axis runs over, the one named last changes fastest.
Arguments:
- activations: bfloat16 [512, 16384], P(None, 'wide'), may hold values from -6 to 6
- enc_weight: bfloat16 [16384, 4096], P('wide', 'narrow'), may hold values from -0.046875 to 0.046875
- enc_bias: float32 [4096], P('narrow'), may hold values from -4 to 4
- dec_weight: bfloat16 [4096, 16384], P('narrow', 'wide'), may hold values from -0.375 to 0.375
- dec_bias: float32 [16384], P('wide'), may hold values from -4 to 4
- active_ids: int32 [512, 64], replicated, may hold values from 0 to 4095, all different within a row
Outputs:
- dec_grad: bfloat16 [4096, 16384], P('narrow', 'wide')
- latent_grad: float32 [512, 4096], P('wide', 'narrow')
Inputs may be any that keep to these rules, and one draw needn't show every extreme that they name: `active_ids`: each row names 64 different latents; every latent is named by some row.
All inputs are finite; a program needn't handle non-finite values.
Results may differ from a plain program's by a relative error of at most 0.0058.
Values may be sent and summed in bfloat16 or wider, within the bound.
A program may use at most 128 MiB of HBM per device.

v0:
```python
import jax
import jax.numpy as jnp
from jax import lax
from jax.sharding import PartitionSpec as P


def prefix(value, axis, combine, identity):
    length, position = (lax.axis_size(axis), lax.axis_index(axis))
    everything = jax.tree.map(
        lambda part, kind: lax.all_gather(part.astype(kind), axis),
        value,
        (jnp.bfloat16, jnp.bfloat16),
    )
    start = jax.tree.map(
        lambda part, zero: jnp.broadcast_to(jnp.asarray(zero, part.dtype), part.shape),
        value,
        identity,
    )

    def hop(k, before):
        reached = k < position
        new = combine(
            before, jax.tree.map(lambda part, own: part[k].astype(own.dtype), everything, value)
        )
        return jax.tree.map(lambda a, b: jnp.where(reached, a, b), new, before)

    return lax.fori_loop(0, length, hop, start)


def add_fields(earlier, later):
    return jax.tree.map(jnp.add, earlier, later)


def local(activations, enc_weight, enc_bias, dec_weight, dec_bias, active_ids):
    token_count = activations.shape[0]
    latent_width = enc_weight.shape[1]
    groups = lax.axis_size("narrow")
    group_index = lax.axis_index("narrow")
    first_latent = group_index * latent_width
    inside = (active_ids >= first_latent) & (active_ids < first_latent + latent_width)
    local_ids = jnp.where(inside, active_ids - first_latent, latent_width)
    row_index = jnp.arange(token_count, dtype=jnp.int32)[:, None]
    active_mask = (
        jnp.zeros((token_count, latent_width), jnp.float32)
        .at[row_index, local_ids]
        .set(1.0, mode="drop")
    )
    share_rows = token_count // lax.axis_size("wide")
    offset = lax.axis_index("wide") * share_rows
    own_mask = lax.dynamic_slice_in_dim(active_mask, offset, share_rows, 0)
    partial_pre = jnp.dot(activations, enc_weight, preferred_element_type=jnp.float32)
    preact = lax.psum(partial_pre, "wide") + enc_bias
    latents = (active_mask * preact).astype(jnp.bfloat16)
    recon_part = jnp.dot(latents, dec_weight, preferred_element_type=jnp.float32)
    target = activations.astype(jnp.float32)
    nothing = jnp.zeros_like(recon_part)
    position = group_index.astype(jnp.float32)
    lower_sum, lower_weighted = prefix(
        (recon_part, position * recon_part), "narrow", add_fields, (nothing, nothing)
    )
    weighted_sum = lax.psum((groups - position) * recon_part, "narrow")
    suffix = (
        (groups - position) * dec_bias
        + weighted_sum
        - position * lower_sum
        + lower_weighted
        - (groups - position) * target
    )
    errors = (suffix / groups).astype(jnp.bfloat16)
    dec_grad = lax.dot_general(
        latents, errors, (((0,), (0,)), ((), ())), preferred_element_type=jnp.float32
    ).astype(jnp.bfloat16)
    latent_rows = lax.psum_scatter(
        lax.dot_general(
            errors, dec_weight, (((1,), (1,)), ((), ())), preferred_element_type=jnp.float32
        ),
        "wide",
        scatter_dimension=0,
        tiled=True,
    )
    latent_out = own_mask * latent_rows
    return (dec_grad, latent_out)


def solution(mesh):
    in_specs = (
        P(None, "wide"),
        P("wide", "narrow"),
        P("narrow"),
        P("narrow", "wide"),
        P("wide"),
        P(),
    )
    out_specs = (P("narrow", "wide"), P("wide", "narrow"))
    return jax.shard_map(local, mesh=mesh, in_specs=in_specs, out_specs=out_specs, check_vma=False)
```

profile of v0, /device:TPU:0, one launch (start us, length us, event | category | flops | bytes accessed | tf_op | source)
XLA Modules:
  0.0 489.2 jit_solution(10238089520648462262)
XLA Ops:
  7.2 0.0 copy-start.5
  7.2 0.0 copy-start.4
  7.2 0.0 copy-start.1
  7.2 0.0 all-reduce.3.cloned.1.call-start
  7.2 6.5 %fusion.3 = f32[512,1024]{1,0:T(8,128)} fusion(bf16[512,2048]{1,0:T(8,128)(2,1)} %param.8, bf16[2048,1024]{1,0:T(8,128)(2,1)} %param.9), kind=kOutput, calls=%fused_computation.18 | convolution fusion | flops 2147483648 | bytes 8388608 | tf_op jit(solution)/shard_map/dot_general | solution.py:51
  13.7 0.0 all-reduce.3.cloned.1.call-update
  13.8 0.0 all-gather.5.cloned.1.call-start
  13.8 0.0 copy-done.1
  13.9 0.0 copy-start.3
  13.9 0.0 copy-done.5
  13.9 0.1 multiply_reduce_fusion
  14.0 0.0 copy-done.4
  14.0 0.1 and_reduce_fusion
  14.2 0.1 copy.8
  14.3 0.1 reshape.18
  14.4 121.4 %scatter_custom_fusion = f32[524288]{0:T(1024)} fusion(s32[32768]{0:T(1024)S(1)} %reshape.18, f32[32768]{0:T(1024)S(1)} %broadcast.15, f32[]{:T(128)} %constant.43.clone.1), kind=kCustom, calls=%fused_computation.8 | custom fusion | bytes 2097156
  135.9 1.7 reshape.15
  137.6 0.0 all-reduce.3.cloned.1.call-done
  137.6 0.0 copy-done.3
  137.6 0.0 copy-start.6
  137.7 2.2 multiply_convert_fusion.2
  139.9 0.6 copy-done.6
  140.5 5.6 %broadcast_multiply_fusion = (f32[512,2048]{1,0:T(8,128)}, bf16[512,2048]{1,0:T(8,128)(2,1)}, bf16[512,2048]{1,0:T(8,128)(2,1)}) fusion(f32[]{:T(128)S(6)} %sub.16, f32[]{:T(128)S(6)} %convert_element_type.42, bf16[512,1024]{1,0:T(8,128)(2,1)S(1)} %multiply_convert_fusion.2, bf16[1024,2048]{1,0:T(8,128)(2,1)S(1)} %copy-done.6), kind=kOutput, calls=%fused_computation.6 | convolution fusion | flops 2151677952 | bytes 13631496 | tf_op jit(solution)/shard_map/dot_general | solution.py:54
  146.1 0.0 copy-start.2
  146.1 0.0 all-gather.5.cloned.1.call-update
  146.1 0.0 all-gather.7.cloned.1.call-start
  146.2 0.7 all-gather.7.cloned.1.call-update
  146.9 0.0 all-reduce.5.cloned.1.call-start
  146.9 0.5 all-reduce.5.cloned.1.call-update
  147.4 0.2 reduce-scatter.2.cloned.1.call-start
  147.7 0.0 copy-done.2
  147.7 88.8 %all-gather.5.cloned.1.call-done = bf16[2048,2048]{1,0:T(8,128)(2,1)} async-done(((bf16[512,2048]{1,0:T(8,128)(2,1)}), bf16[2048,2048]{1,0:T(8,128)(2,1)}) %all-gather.5.cloned.1.call-update) | async-done | bytes 8388624 | tf_op jit(solution)/shard_map/all_gather | solution.py:10
  236.5 89.4 %all-gather.7.cloned.1.call-done = bf16[2048,2048]{1,0:T(8,128)(2,1)} async-done(((bf16[512,2048]{1,0:T(8,128)(2,1)}), bf16[2048,2048]{1,0:T(8,128)(2,1)}) %all-gather.7.cloned.1.call-update) | async-done | bytes 8388624 | tf_op jit(solution)/shard_map/all_gather | solution.py:10
  325.8 39.3 %while.16 = (s32[]{:T(128)}, f32[512,2048]{1,0:T(8,128)}, f32[512,2048]{1,0:T(8,128)}, s32[]{:T(128)}, bf16[4,512,2048]{2,1,0:T(8,128)(2,1)}, /*index=5*/bf16[4,512,2048]{2,1,0:T(8,128)(2,1)}, s32[]{:T(128)}, s32[]{:T(128)}) while((s32[]{:T(128)}, f32[512,2048]{1,0:T(8,128)}, f32[512,2048]{1,0:T(8,128)}, s32[]{:T(128)}, ...), condition=%wide.region_4.5_spmd.clone, body=%wide.region_3.4_spmd.clone.sunk | while | flops 8388612 | bytes 20971628 | solution.py:27
  325.8 7.8 %add_select_fusion.3 = (f32[512,2048]{1,0:T(8,128)}, f32[512,2048]{1,0:T(8,128)}) fusion(f32[512,2048]{1,0:T(8,128)} %get-tuple-element.204, bf16[4,512,2048]{2,1,0:T(8,128)(2,1)} %get-tuple-element.215, s32[]{:T(128)} %get-tuple-element.202, pred[]{:T(512)S(6)} %compare.7, pred[]{:T(512)S(6)} %lt.50, bf16[4,512,2048]{2,1,0:T(8,128)(2,1)} %get-tuple-element.214, ...), kind=kLoop, calls=%fused_computation.1.clone.1 | loop fusion | flops 8388608 | bytes 20971526 | tf_op jit(solution)/shard_map/while/body/eval_jaxpr/jit(_where)/select_n | solution.py:25
  333.6 10.8 %add_select_fusion.3 = (f32[512,2048]{1,0:T(8,128)}, f32[512,2048]{1,0:T(8,128)}) fusion(f32[512,2048]{1,0:T(8,128)} %get-tuple-element.204, bf16[4,512,2048]{2,1,0:T(8,128)(2,1)} %get-tuple-element.215, s32[]{:T(128)} %get-tuple-element.202, pred[]{:T(512)S(6)} %compare.7, pred[]{:T(512)S(6)} %lt.50, bf16[4,512,2048]{2,1,0:T(8,128)(2,1)} %get-tuple-element.214, ...), kind=kLoop, calls=%fused_computation.1.clone.1 | loop fusion | flops 8388608 | bytes 20971526 | tf_op jit(solution)/shard_map/while/body/eval_jaxpr/jit(_where)/select_n | solution.py:25
  344.4 10.4 %add_select_fusion.3 = (f32[512,2048]{1,0:T(8,128)}, f32[512,2048]{1,0:T(8,128)}) fusion(f32[512,2048]{1,0:T(8,128)} %get-tuple-element.204, bf16[4,512,2048]{2,1,0:T(8,128)(2,1)} %get-tuple-element.215, s32[]{:T(128)} %get-tuple-element.202, pred[]{:T(512)S(6)} %compare.7, pred[]{:T(512)S(6)} %lt.50, bf16[4,512,2048]{2,1,0:T(8,128)(2,1)} %get-tuple-element.214, ...), kind=kLoop, calls=%fused_computation.1.clone.1 | loop fusion | flops 8388608 | bytes 20971526 | tf_op jit(solution)/shard_map/while/body/eval_jaxpr/jit(_where)/select_n | solution.py:25
  354.8 10.3 %add_select_fusion.3 = (f32[512,2048]{1,0:T(8,128)}, f32[512,2048]{1,0:T(8,128)}) fusion(f32[512,2048]{1,0:T(8,128)} %get-tuple-element.204, bf16[4,512,2048]{2,1,0:T(8,128)(2,1)} %get-tuple-element.215, s32[]{:T(128)} %get-tuple-element.202, pred[]{:T(512)S(6)} %compare.7, pred[]{:T(512)S(6)} %lt.50, bf16[4,512,2048]{2,1,0:T(8,128)(2,1)} %get-tuple-element.214, ...), kind=kLoop, calls=%fused_computation.1.clone.1 | loop fusion | flops 8388608 | bytes 20971526 | tf_op jit(solution)/shard_map/while/body/eval_jaxpr/jit(_where)/select_n | solution.py:25
  365.1 67.5 %all-reduce.5.cloned.1.call-done = f32[512,2048]{1,0:T(8,128)} async-done(((f32[512,2048]{1,0:T(8,128)}), f32[512,2048]{1,0:T(8,128)}) %all-reduce.5.cloned.1.call-update) | async-done | bytes 4194320 | tf_op jit(solution)/shard_map/psum | solution.py:61
  432.6 0.0 copy-start.7
  432.6 7.2 %multiply_convert_fusion = bf16[512,2048]{1,0:T(8,128)(2,1)S(1)} fusion(bf16[512,2048]{1,0:T(8,128)(2,1)} %param.8, f32[512,2048]{1,0:T(8,128)} %get-tuple-element.113, f32[512,2048]{1,0:T(8,128)} %get-tuple-element.112, f32[512,2048]{1,0:T(8,128)} %all-reduce.5.cloned.1.call-done, f32[]{:T(128)S(6)} %convert_element_type.42, f32[]{:T(128)S(6)} %sub.16, ...), kind=kLoop, calls=%fused_computation.3 | loop fusion | flops 9437184 | bytes 16785416 | tf_op jit(solution)/shard_map/convert_element_type | solution.py:69
  439.8 0.0 copy-start
  439.8 1.3 copy-done
  441.1 0.0 copy-done.7
  441.1 3.7 fusion.4
  444.8 0.0 reduce-scatter.2.cloned.1.call-update
  444.8 6.0 %convolution_convert_fusion = bf16[1024,2048]{1,0:T(8,128)(2,1)} fusion(bf16[512,1024]{1,0:T(8,128)(2,1)S(1)} %multiply_convert_fusion.2, bf16[512,2048]{1,0:T(8,128)(2,1)} %copy-done), kind=kOutput, calls=%fused_computation.5 | convolution fusion | flops 2149580800 | bytes 7340032 | tf_op jit(solution)/shard_map/dot_general | solution.py:70
  450.8 30.2 %reduce-scatter.2.cloned.1.call-done = f32[64,1024]{1,0:T(8,128)} async-done(((f32[512,1024]{1,0:T(8,128)}), f32[64,1024]{1,0:T(8,128)}) %reduce-scatter.2.cloned.1.call-update) | async-done | bytes 262160 | tf_op jit(solution)/shard_map/reduce_scatter | solution.py:73
  481.0 1.7 dynamic-slice_multiply_fusion
  (7 shorter events, 0.1 us)
Async XLA Ops:
  7.2 6.8 %copy-start.5 = (s32[2]{0:T(128)S(1)}, s32[2]{0:T(128)}, u32[]{:S(2)}) copy-start(s32[2]{0:T(128)} %constant.54) | copy-start | bytes 28
  7.2 6.8 %copy-start.4 = (s32[2]{0:T(128)S(1)}, s32[2]{0:T(128)}, u32[]{:S(2)}) copy-start(s32[2]{0:T(128)} %constant.57) | copy-start | bytes 28
  7.2 6.6 %copy-start.1 = (s32[512,64]{0,1:T(8,128)S(1)}, s32[512,64]{0,1:T(8,128)}, u32[]{:S(2)}) copy-start(s32[512,64]{0,1:T(8,128)} %param.13) | copy-start | bytes 393220
  7.2 130.4 %all-reduce.3.cloned.1.call-start = ((), (), s32[]{:S(2)}) async-start(), calls=%async_computation.1 | async-start | bytes 4194304 | tf_op jit(solution)/shard_map/psum | solution.py:52
  13.8 222.7 %all-gather.5.cloned.1.call-start = ((), (), s32[]{:S(2)}) async-start(), calls=%async_computation.4 | async-start | bytes 10485760 | tf_op jit(solution)/shard_map/all_gather | solution.py:10
  13.9 123.8 %copy-start.3 = (f32[1024]{0:T(1024)S(1)}, f32[1024]{0:T(1024)}, u32[]{:S(2)}) copy-start(f32[1024]{0:T(1024)} %param.10) | copy-start | bytes 12292
  137.6 2.8 copy-start.6
  146.1 1.6 copy-start.2
  146.1 179.7 %all-gather.7.cloned.1.call-start = ((), (), s32[]{:S(2)}) async-start(), calls=%async_computation.5 | async-start | bytes 10485760 | tf_op jit(solution)/shard_map/all_gather | solution.py:10
  146.9 285.8 %all-reduce.5.cloned.1.call-start = ((), (), s32[]{:S(2)}) async-start(), calls=%async_computation.2 | async-start | bytes 8388608 | tf_op jit(solution)/shard_map/psum | solution.py:61
  147.4 333.6 %reduce-scatter.2.cloned.1.call-start = ((), (), s32[]{:S(2)}) async-start(), calls=%async_computation.3 | async-start | bytes 2359296 | tf_op jit(solution)/shard_map/reduce_scatter | solution.py:73
  432.6 8.5 %copy-start.7 = (bf16[1024,2048]{1,0:T(8,128)(2,1)S(1)}, bf16[1024,2048]{1,0:T(8,128)(2,1)}, u32[]{:S(2)}) copy-start(bf16[1024,2048]{1,0:T(8,128)(2,1)} %param.11) | copy-start | bytes 12582916
  439.8 1.3 copy-start
Sparse Core Ops, SparseCore 0:
  13.9 67.9 all-reduce.2
  146.2 90.1 all-gather.4
  238.3 87.4 all-gather.6
  329.0 103.5 all-reduce.4
  445.0 35.9 reduce-scatter.1
where the time goes:
time: 489 us
  waiting for transfers between devices  277 us (57%)
  local copies, waits for them, and re-layouts  125 us (26%)
  other arithmetic  50.6 us (10%)
  matrix products  21.8 us (4%)
  between operations  14 us (3%)
    all_gather x2, waiting for transfers between devices, prefix(): lax.all_gather(part.astype(kind), axis)  178 us
    unnamed x20, local copies, waits for them, and re-layouts  124 us
    psum x1, waiting for transfers between devices, local(): weighted_sum = lax.psum((groups - position) * recon_part, 'narrow')  67.5 us
    select_n x4, other arithmetic, hop(): return jax.tree.map(lambda a, b: jnp.where(reached, a, b), new, before)  39.3 us
    reduce_scatter x1, waiting for transfers between devices, local(): lax.psum_scatter(lax.dot_general(errors, dec_weight, (((1,), (1,)), ((),...  30.2 us
  transfers between devices with their start and end apart: 5, of which 4 were waited for; matrix products, arithmetic and copies ran while one was open for 35% of the time, Pallas kernels for 0%

commit v1 on v0

--- a/solution.py
+++ b/solution.py
@@ -2,6 +2,7 @@
 import jax.numpy as jnp
 from jax import lax
 from jax.sharding import PartitionSpec as P
+from jax.lax import all_gather
 
 
 def prefix(value, axis, combine, identity):
@@ -32,6 +33,12 @@
 
 
 def local(activations, enc_weight, enc_bias, dec_weight, dec_bias, active_ids):
+
+    def knots_treat(frame_in, link_axis="narrow"):
+        near = all_gather(frame_in, link_axis)
+        carry = jnp.sum(near, axis=0)
+        return carry
+
     token_count = activations.shape[0]
     latent_width = enc_weight.shape[1]
     groups = lax.axis_size("narrow")
@@ -58,7 +65,7 @@
     lower_sum, lower_weighted = prefix(
         (recon_part, position * recon_part), "narrow", add_fields, (nothing, nothing)
     )
-    weighted_sum = lax.psum((groups - position) * recon_part, "narrow")
+    weighted_sum = knots_treat((groups - position) * recon_part)
     suffix = (
         (groups - position) * dec_bias
         + weighted_sum

time: 489 us -> 552 us (1.13)
  waiting for transfers between devices: 277 us -> 328 us
  other arithmetic: 50.6 us -> 62.3 us
    all_gather x0 -> x1, waiting for transfers between devices: none -> 118 us  [knots_treat(): near = all_gather(frame_in, link_axis)]
    psum x1 -> x0, waiting for transfers between devices: 67.5 us -> none  [local(): weighted_sum = lax.psum((groups - position) * recon_part, 'narrow')]
    reduce_sum x0 -> x1, other arithmetic: none -> 10.1 us  [knots_treat(): carry = jnp.sum(near, axis=0)]
  transfers between devices with their start and end apart: 5 -> 5, of which waited for: 4 -> 4; matrix products, arithmetic and copies ran while one was open for 35% -> 31% of each run, Pallas kernels for 0% -> 0%
where the time goes in v1:
time: 552 us
  waiting for transfers between devices  328 us (59%)
  local copies, waits for them, and re-layouts  125 us (23%)
  other arithmetic  62.3 us (11%)
  matrix products  21.9 us (4%)
  between operations  14 us (3%)
    all_gather x2, waiting for transfers between devices, prefix(): lax.all_gather(part.astype(kind), axis)  178 us
    unnamed x20, local copies, waits for them, and re-layouts  124 us
    all_gather x1, waiting for transfers between devices, knots_treat(): near = all_gather(frame_in, link_axis)  118 us
    select_n x4, other arithmetic, hop(): return jax.tree.map(lambda a, b: jnp.where(reached, a, b), new, before)  40.8 us
    reduce_scatter x1, waiting for transfers between devices, local(): lax.psum_scatter(lax.dot_general(errors, dec_weight, (((1,), (1,)), ((),...  30.2 us
  transfers between devices with their start and end apart: 5, of which 4 were waited for; matrix products, arithmetic and copies ran while one was open for 31% of the time, Pallas kernels for 0%

profile of v1, /device:TPU:0, one launch (start us, length us, event | category | flops | bytes accessed | tf_op | source)
XLA Modules:
  0.0 551.7 jit_solution(18410821786554459092)
XLA Ops:
  7.2 0.0 copy-start.5
  7.2 0.0 copy-start.4
  7.2 0.0 copy-start.1
  7.2 0.0 all-reduce.2.cloned.1.call-start
  7.2 6.5 %fusion.3 = f32[512,1024]{1,0:T(8,128)} fusion(bf16[512,2048]{1,0:T(8,128)(2,1)} %param.8, bf16[2048,1024]{1,0:T(8,128)(2,1)} %param.9), kind=kOutput, calls=%fused_computation.18 | convolution fusion | flops 2147483648 | bytes 8388608 | tf_op jit(solution)/shard_map/dot_general | solution.py:58
  13.7 0.0 all-reduce.2.cloned.1.call-update
  13.8 0.0 all-gather.9.cloned.1.call-start
  13.8 0.0 copy-done.1
  13.9 0.0 copy-start.3
  13.9 0.0 copy-done.5
  13.9 0.1 multiply_reduce_fusion
  14.0 0.0 copy-done.4
  14.0 0.1 and_reduce_fusion
  14.2 0.1 copy.8
  14.3 0.1 reshape.18
  14.4 121.4 %scatter_custom_fusion = f32[524288]{0:T(1024)} fusion(s32[32768]{0:T(1024)S(1)} %reshape.18, f32[32768]{0:T(1024)S(1)} %broadcast.15, f32[]{:T(128)} %constant.44.clone.1), kind=kCustom, calls=%fused_computation.8 | custom fusion | bytes 2097156
  135.9 1.7 reshape.15
  137.6 0.0 all-reduce.2.cloned.1.call-done
  137.6 0.0 copy-done.3
  137.6 0.0 copy-start.6
  137.7 2.2 multiply_convert_fusion.2
  139.9 0.6 copy-done.6
  140.5 5.7 %broadcast_multiply_fusion = (f32[512,2048]{1,0:T(8,128)}, bf16[512,2048]{1,0:T(8,128)(2,1)}, bf16[512,2048]{1,0:T(8,128)(2,1)}) fusion(f32[]{:T(128)S(6)} %sub.16, f32[]{:T(128)S(6)} %convert_element_type.42, bf16[512,1024]{1,0:T(8,128)(2,1)S(1)} %multiply_convert_fusion.2, bf16[1024,2048]{1,0:T(8,128)(2,1)S(1)} %copy-done.6), kind=kOutput, calls=%fused_computation.6 | convolution fusion | flops 2151677952 | bytes 13631496 | tf_op jit(solution)/shard_map/dot_general | solution.py:61
  146.2 0.0 copy-start.2
  146.2 0.0 all-gather.9.cloned.1.call-update
  146.2 0.0 all-gather.11.cloned.1.call-start
  146.2 0.7 all-gather.11.cloned.1.call-update
  146.9 0.0 all-gather.7.cloned.1.call-start
  147.0 0.5 all-gather.7.cloned.1.call-update
  147.5 0.2 reduce-scatter.2.cloned.1.call-start
  147.7 0.0 copy-done.2
  147.8 88.8 %all-gather.9.cloned.1.call-done = bf16[2048,2048]{1,0:T(8,128)(2,1)} async-done(((bf16[512,2048]{1,0:T(8,128)(2,1)}), bf16[2048,2048]{1,0:T(8,128)(2,1)}) %all-gather.9.cloned.1.call-update) | async-done | bytes 8388624 | tf_op jit(solution)/shard_map/all_gather | solution.py:11
  236.5 89.4 %all-gather.11.cloned.1.call-done = bf16[2048,2048]{1,0:T(8,128)(2,1)} async-done(((bf16[512,2048]{1,0:T(8,128)(2,1)}), bf16[2048,2048]{1,0:T(8,128)(2,1)}) %all-gather.11.cloned.1.call-update) | async-done | bytes 8388624 | tf_op jit(solution)/shard_map/all_gather | solution.py:11
  325.9 40.8 %while.16 = (s32[]{:T(128)}, f32[512,2048]{1,0:T(8,128)}, f32[512,2048]{1,0:T(8,128)}, s32[]{:T(128)}, bf16[4,512,2048]{2,1,0:T(8,128)(2,1)}, /*index=5*/bf16[4,512,2048]{2,1,0:T(8,128)(2,1)}, s32[]{:T(128)}, s32[]{:T(128)}) while((s32[]{:T(128)}, f32[512,2048]{1,0:T(8,128)}, f32[512,2048]{1,0:T(8,128)}, s32[]{:T(128)}, ...), condition=%wide.region_4.5_spmd.clone, body=%wide.region_3.4_spmd.clone.sunk | while | flops 8388612 | bytes 20971628 | solution.py:28
  325.9 7.8 %add_select_fusion.3 = (f32[512,2048]{1,0:T(8,128)}, f32[512,2048]{1,0:T(8,128)}) fusion(f32[512,2048]{1,0:T(8,128)} %get-tuple-element.204, bf16[4,512,2048]{2,1,0:T(8,128)(2,1)} %get-tuple-element.215, s32[]{:T(128)} %get-tuple-element.202, pred[]{:T(512)S(6)} %compare.7, pred[]{:T(512)S(6)} %lt.50, bf16[4,512,2048]{2,1,0:T(8,128)(2,1)} %get-tuple-element.214, ...), kind=kLoop, calls=%fused_computation.1.clone.1 | loop fusion | flops 8388608 | bytes 20971526 | tf_op jit(solution)/shard_map/while/body/eval_jaxpr/jit(_where)/select_n | solution.py:26
  333.7 12.7 %add_select_fusion.3 = (f32[512,2048]{1,0:T(8,128)}, f32[512,2048]{1,0:T(8,128)}) fusion(f32[512,2048]{1,0:T(8,128)} %get-tuple-element.204, bf16[4,512,2048]{2,1,0:T(8,128)(2,1)} %get-tuple-element.215, s32[]{:T(128)} %get-tuple-element.202, pred[]{:T(512)S(6)} %compare.7, pred[]{:T(512)S(6)} %lt.50, bf16[4,512,2048]{2,1,0:T(8,128)(2,1)} %get-tuple-element.214, ...), kind=kLoop, calls=%fused_computation.1.clone.1 | loop fusion | flops 8388608 | bytes 20971526 | tf_op jit(solution)/shard_map/while/body/eval_jaxpr/jit(_where)/select_n | solution.py:26
  346.3 10.2 %add_select_fusion.3 = (f32[512,2048]{1,0:T(8,128)}, f32[512,2048]{1,0:T(8,128)}) fusion(f32[512,2048]{1,0:T(8,128)} %get-tuple-element.204, bf16[4,512,2048]{2,1,0:T(8,128)(2,1)} %get-tuple-element.215, s32[]{:T(128)} %get-tuple-element.202, pred[]{:T(512)S(6)} %compare.7, pred[]{:T(512)S(6)} %lt.50, bf16[4,512,2048]{2,1,0:T(8,128)(2,1)} %get-tuple-element.214, ...), kind=kLoop, calls=%fused_computation.1.clone.1 | loop fusion | flops 8388608 | bytes 20971526 | tf_op jit(solution)/shard_map/while/body/eval_jaxpr/jit(_where)/select_n | solution.py:26
  356.5 10.2 %add_select_fusion.3 = (f32[512,2048]{1,0:T(8,128)}, f32[512,2048]{1,0:T(8,128)}) fusion(f32[512,2048]{1,0:T(8,128)} %get-tuple-element.204, bf16[4,512,2048]{2,1,0:T(8,128)(2,1)} %get-tuple-element.215, s32[]{:T(128)} %get-tuple-element.202, pred[]{:T(512)S(6)} %compare.7, pred[]{:T(512)S(6)} %lt.50, bf16[4,512,2048]{2,1,0:T(8,128)(2,1)} %get-tuple-element.214, ...), kind=kLoop, calls=%fused_computation.1.clone.1 | loop fusion | flops 8388608 | bytes 20971526 | tf_op jit(solution)/shard_map/while/body/eval_jaxpr/jit(_where)/select_n | solution.py:26
  366.7 118.2 %all-gather.7.cloned.1.call-done = f32[2048,2048]{1,0:T(8,128)} async-done(((f32[512,2048]{1,0:T(8,128)}), f32[2048,2048]{1,0:T(8,128)}) %all-gather.7.cloned.1.call-update) | async-done | bytes 16777232 | tf_op jit(solution)/shard_map/all_gather | solution.py:38
  484.9 10.1 %reduce_sum.9 = f32[512,2048]{1,0:T(8,128)} reduce(f32[4,512,2048]{2,1,0:T(8,128)} %bitcast.21, f32[]{:T(128)} %constant.44.clone.1), dimensions={0}, to_apply=%region_2.3 | reduce | flops 3145728 | bytes 20971524 | tf_op jit(solution)/shard_map/reduce_sum | solution.py:39
  495.0 0.0 copy-start.7
  495.0 7.2 %multiply_convert_fusion = bf16[512,2048]{1,0:T(8,128)(2,1)S(1)} fusion(bf16[512,2048]{1,0:T(8,128)(2,1)} %param.8, f32[512,2048]{1,0:T(8,128)} %get-tuple-element.113, f32[512,2048]{1,0:T(8,128)} %get-tuple-element.112, f32[512,2048]{1,0:T(8,128)} %reduce_sum.9, f32[]{:T(128)S(6)} %convert_element_type.42, f32[]{:T(128)S(6)} %sub.16, ...), kind=kLoop, calls=%fused_computation.3 | loop fusion | flops 9437184 | bytes 16785416 | tf_op jit(solution)/shard_map/convert_element_type | solution.py:76
  502.2 0.0 copy-start
  502.2 1.3 copy-done
  503.5 0.0 copy-done.7
  503.5 3.7 fusion.4
  507.2 0.0 reduce-scatter.2.cloned.1.call-update
  507.3 6.0 %convolution_convert_fusion = bf16[1024,2048]{1,0:T(8,128)(2,1)} fusion(bf16[512,1024]{1,0:T(8,128)(2,1)S(1)} %multiply_convert_fusion.2, bf16[512,2048]{1,0:T(8,128)(2,1)} %copy-done), kind=kOutput, calls=%fused_computation.5 | convolution fusion | flops 2149580800 | bytes 7340032 | tf_op jit(solution)/shard_map/dot_general | solution.py:77
  513.3 30.2 %reduce-scatter.2.cloned.1.call-done = f32[64,1024]{1,0:T(8,128)} async-done(((f32[512,1024]{1,0:T(8,128)}), f32[64,1024]{1,0:T(8,128)}) %reduce-scatter.2.cloned.1.call-update) | async-done | bytes 262160 | tf_op jit(solution)/shard_map/reduce_scatter | solution.py:80
  543.5 1.7 dynamic-slice_multiply_fusion
  (7 shorter events, 0.1 us)
Async XLA Ops:
  7.2 6.8 %copy-start.5 = (s32[2]{0:T(128)S(1)}, s32[2]{0:T(128)}, u32[]{:S(2)}) copy-start(s32[2]{0:T(128)} %constant.55) | copy-start | bytes 28
  7.2 6.8 %copy-start.4 = (s32[2]{0:T(128)S(1)}, s32[2]{0:T(128)}, u32[]{:S(2)}) copy-start(s32[2]{0:T(128)} %constant.58) | copy-start | bytes 28
  7.2 6.6 %copy-start.1 = (s32[512,64]{0,1:T(8,128)S(1)}, s32[512,64]{0,1:T(8,128)}, u32[]{:S(2)}) copy-start(s32[512,64]{0,1:T(8,128)} %param.13) | copy-start | bytes 393220
  7.2 130.4 %all-reduce.2.cloned.1.call-start = ((), (), s32[]{:S(2)}) async-start(), calls=%async_computation.1 | async-start | bytes 4194304 | tf_op jit(solution)/shard_map/psum | solution.py:59
  13.8 222.8 %all-gather.9.cloned.1.call-start = ((), (), s32[]{:S(2)}) async-start(), calls=%async_computation.4 | async-start | bytes 10485760 | tf_op jit(solution)/shard_map/all_gather | solution.py:11
  13.9 123.8 %copy-start.3 = (f32[1024]{0:T(1024)S(1)}, f32[1024]{0:T(1024)}, u32[]{:S(2)}) copy-start(f32[1024]{0:T(1024)} %param.10) | copy-start | bytes 12292
  137.6 2.8 copy-start.6
  146.2 1.6 copy-start.2
  146.2 179.7 %all-gather.11.cloned.1.call-start = ((), (), s32[]{:S(2)}) async-start(), calls=%async_computation.5 | async-start | bytes 10485760 | tf_op jit(solution)/shard_map/all_gather | solution.py:11
  146.9 338.0 %all-gather.7.cloned.1.call-start = ((), (), s32[]{:S(2)}) async-start(), calls=%async_computation.3 | async-start | bytes 20971520 | tf_op jit(solution)/shard_map/all_gather | solution.py:38
  147.5 396.0 %reduce-scatter.2.cloned.1.call-start = ((), (), s32[]{:S(2)}) async-start(), calls=%async_computation.2 | async-start | bytes 2359296 | tf_op jit(solution)/shard_map/reduce_scatter | solution.py:80
  495.0 8.5 %copy-start.7 = (bf16[1024,2048]{1,0:T(8,128)(2,1)S(1)}, bf16[1024,2048]{1,0:T(8,128)(2,1)}, u32[]{:S(2)}) copy-start(bf16[1024,2048]{1,0:T(8,128)(2,1)} %param.11) | copy-start | bytes 12582916
  502.2 1.3 copy-start
Sparse Core Ops, SparseCore 0:
  13.9 67.9 all-reduce.1
  146.3 90.1 all-gather.8
  238.4 87.4 all-gather.10
  327.6 157.2 all-gather.6
  507.4 36.0 reduce-scatter.1
